TPU v7x, 32 devices: a whole 2x2x4 slice. The times are simulated.
32 devices in a mesh: dp: 8 (over z, x), hyper: 4 (over y, core).
Axes of the slice: x: 2, y: 2, z: 4, core: 2. Of those that a mesh axis runs over, the one named last changes fastest.
Arguments:
- inputs: bfloat16 [64, 64, 128], P(('dp', 'hyper')), may hold values from -64 to 64
- labels: int32 [64, 64], P(('dp', 'hyper')), may hold values from 0 to 255
- client_ids: int32 [64], P(('dp', 'hyper')), may hold values from 0 to 63
- ext_weight: bfloat16 [128, 4096], replicated, may hold values from -0.5 to 0.5
- ext_bias: bfloat16 [4096], replicated, may hold values from -3 to 3
- embeddings: bfloat16 [64, 128], replicated, may hold values from -1.5 to 1.5
- hyper_in: bfloat16 [128, 50], replicated, may hold values from -2.09375 to 2.09375
- hyper_bias: float32 [50], replicated, may hold values from -3 to 3
- hyper_out: bfloat16 [4096, 50, 256], P('hyper'), may hold values from -0.1796875 to 0.1796875
Outputs:
- grad_ext_weight: float32 [128, 4096], replicated
- grad_ext_bias: float32 [4096], replicated
- grad_embeddings: float32 [64, 128], replicated
- grad_hyper_in: float32 [128, 50], replicated
- grad_hyper_bias: float32 [50], replicated
- grad_hyper_out: float32 [4096, 50, 256], P(('hyper', 'dp'))
Inputs may be any that keep to these rules, and one draw needn't show every extreme that they name: `client_ids`: A client may hold several slots or none.
All inputs are finite; a program needn't handle non-finite values.
Results may differ from a plain program's by a relative error of at most 0.014.
The roundings to bfloat16 on the way count: a program that leaves them out, or rounds other values in their place, can miss the bound.
Values may be sent and summed in bfloat16 or wider, within the bound.
A program may use at most 192 MiB of HBM per device.

v0:
```python
import jax
import jax.numpy as jnp
from jax import lax
from jax.sharding import PartitionSpec as P

highest = lax.Precision.HIGHEST
f32 = jnp.float32
bf16 = jnp.bfloat16


def silu_slope(values):
    logistic = jax.nn.sigmoid(values)
    return logistic * (1.0 + values * (1.0 - logistic))


def class_grads(logits, slot_labels, row_count):
    largest = jnp.max(logits, axis=-1, keepdims=True)
    exponent = jnp.exp(logits - largest)
    probability = exponent / jnp.sum(exponent, axis=-1, keepdims=True)
    classes = jnp.arange(logits.shape[-1], dtype=jnp.int32)
    onehot = (slot_labels[..., None] == classes).astype(f32)
    return ((probability - onehot) / row_count).astype(bf16)


def local(
    inputs, labels, client_ids, ext_weight, ext_bias, embeddings, hyper_in, hyper_bias, hyper_out
):
    everyone = ("dp", "hyper")
    n_dp, n_hyper = (lax.axis_size("dp"), lax.axis_size("hyper"))
    i, j = (lax.axis_index("dp"), lax.axis_index("hyper"))
    own, rows, width_in = inputs.shape
    wide = hyper_out.shape[0]
    narrow = wide // n_dp
    group = own * n_hyper
    slots = group * n_dp
    classes = hyper_out.shape[2]
    ids = lax.all_gather(client_ids, everyone, axis=0, tiled=True)
    in_group = lax.all_gather(inputs, "hyper", axis=0, tiled=True)
    in_all = lax.all_gather(in_group, "dp", axis=0, tiled=True)
    select = ids[:, None] == jnp.arange(embeddings.shape[0], dtype=jnp.int32)[None, :]
    picked = jnp.dot(select.astype(bf16), embeddings, preferred_element_type=f32).astype(bf16)
    hyper_preact = jnp.dot(picked, hyper_in, preferred_element_type=f32) + hyper_bias
    hidden = jax.nn.silu(hyper_preact).astype(bf16)
    w_wide = lax.dynamic_slice_in_dim(ext_weight, j * wide, wide, 1)
    b_wide = lax.dynamic_slice_in_dim(ext_bias, j * wide, wide, 0).astype(f32)
    preact = jnp.dot(in_group.reshape(group * rows, width_in), w_wide, preferred_element_type=f32)
    features = jax.nn.silu(preact + b_wide).astype(bf16).reshape(group, rows, wide)
    hidden_group = lax.dynamic_slice_in_dim(hidden, i * group, group, 0)
    heads = jnp.einsum("kh,dhc->kdc", hidden_group, hyper_out, preferred_element_type=f32)
    part = jnp.einsum("krd,kdc->krc", features, heads.astype(bf16), preferred_element_type=f32)
    parts = lax.all_to_all(
        part.reshape(n_hyper, own * rows, classes), "hyper", split_axis=0, concat_axis=0
    )
    logits = jnp.sum(parts, axis=0).reshape(own, rows, classes)
    dlogits = class_grads(logits, labels, rows)
    dl_all = lax.all_gather(dlogits, everyone, axis=0, tiled=True)
    start = (j * n_dp + i) * narrow
    w = lax.dynamic_slice_in_dim(ext_weight, start, narrow, 1)
    b = lax.dynamic_slice_in_dim(ext_bias, start, narrow, 0).astype(f32)
    out_rows = lax.dynamic_slice_in_dim(hyper_out, i * narrow, narrow, 0)
    flat = in_all.reshape(slots * rows, width_in)
    preact = jnp.dot(flat, w, preferred_element_type=f32) + b
    features = jax.nn.silu(preact).astype(bf16).reshape(slots, rows, narrow)
    heads = jnp.einsum("kh,dhc->kdc", hidden, out_rows, preferred_element_type=f32).astype(bf16)
    dheads = jnp.einsum("krd,krc->kdc", features, dl_all, preferred_element_type=f32).astype(bf16)
    dfeatures = jnp.einsum("krc,kdc->krd", dl_all, heads, preferred_element_type=f32).astype(bf16)
    dpreact = (dfeatures.reshape(slots * rows, narrow).astype(f32) * silu_slope(preact)).astype(
        bf16
    )
    grad_weight = jnp.dot(flat.T, dpreact, preferred_element_type=f32)
    grad_bias = jnp.sum(dpreact.astype(f32), axis=0)
    grad_out = jnp.einsum("kh,kdc->dhc", hidden, dheads, preferred_element_type=f32)
    dhidden = jnp.einsum("kdc,dhc->kh", dheads, out_rows, preferred_element_type=f32)
    dhidden = lax.psum(dhidden, everyone)
    hyper_dpre = dhidden * silu_slope(hyper_preact)
    grad_in = jnp.dot(picked.astype(f32).T, hyper_dpre, precision=highest)
    grad_hbias = jnp.sum(hyper_dpre, axis=0)
    back_rows = jnp.dot(hyper_dpre, hyper_in.astype(f32).T, precision=highest)
    grad_table = jnp.dot(select.astype(f32).T, back_rows, precision=highest)
    both = jnp.concatenate([grad_weight, grad_bias[None]], axis=0)
    both = lax.all_gather(both, ("hyper", "dp"), axis=1, tiled=True)
    return (both[:-1], both[-1], grad_table, grad_in, grad_hbias, grad_out)


def solution(mesh):
    placed = (
        P(("dp", "hyper"), None, None),
        P(("dp", "hyper"), None),
        P(("dp", "hyper")),
        P(),
        P(),
        P(),
        P(),
        P(),
        P("hyper", None, None),
    )
    return jax.shard_map(
        local,
        mesh=mesh,
        in_specs=placed,
        out_specs=(P(), P(), P(), P(), P(), P(("hyper", "dp"), None, None)),
        check_vma=False,
    )
```

profile of v0, /device:TPU:0, one launch (start us, length us, event | category | flops | bytes accessed | tf_op | source)
XLA Modules:
  0.0 276.0 jit_solution(7571744221663631513)
XLA Ops:
  7.2 0.0 copy-start
  7.2 0.0 all-gather.4.cloned.1.call-start
  7.2 0.9 dynamic-update-slice
  8.2 42.0 %all-reduce = s32[64]{0:T(128)S(1)} all-reduce(s32[64]{0:T(128)S(1)} %dynamic-update-slice), channel_id=1, replica_groups=mesh['dp'=8,'hyper'=4] {'dp','hyper'}, use_global_device_ids=true, to_apply=%add | all-reduce | flops 64 | bytes 512
  50.1 6.0 %all_gather.15 = bf16[8,64,128]{2,1,0:T(8,128)(2,1)S(1)} all-gather(bf16[2,64,128]{2,1,0:T(8,128)(2,1)} %param.9), channel_id=1, replica_groups=mesh['dp'=8,'hyper'=4] {'hyper'}, dimensions={0}, use_global_device_ids=true | all-gather | bytes 163840 | tf_op jit(solution)/shard_map/all_gather | solution.py:38
  56.1 0.7 dynamic-slice_convert_fusion
  56.8 0.9 convolution_convert_fusion.2
  57.7 0.9 multiply_convert_fusion.3
  58.6 0.7 fusion.21
  59.4 0.0 copy-done.3
  59.4 28.0 %convolution_convert_fusion.1 = bf16[8,1024,256]{2,0,1:T(8,128)(2,1)S(1)} fusion(bf16[64,50]{0,1:T(8,128)(2,1)S(1)} %get-tuple-element.29, s32[]{:T(128)S(6)} %select_n.15, bf16[1024,50,256]{2,0,1:T(8,128)(2,1)} %param.17), kind=kOutput, calls=%fused_computation.16 | convolution fusion | flops 211812352 | bytes 30415108 | tf_op jit(solution)/shard_map/kh,dhc->kdc/dot_general | solution.py:49
  87.4 0.0 copy-start.5
  87.4 0.9 fusion.3
  88.2 11.8 %all_to_all.5 = f32[4,128,256]{2,1,0:T(8,128)S(1)} all-to-all(f32[4,128,256]{2,1,0:T(8,128)S(1)} %bitcast.61), channel_id=1, replica_groups=mesh['dp'=8,'hyper'=4] {'hyper'}, dimensions={0} | all-to-all | bytes 1048576 | tf_op jit(solution)/shard_map/all_to_all | solution.py:51
  100.0 0.1 reduce_max.9
  100.1 0.2 exponential_reduce_fusion
  100.3 0.1 sub.24
  100.4 0.1 div.32
  100.5 0.0 copy-done.5
  100.5 0.8 multiply_convert_fusion.2
  101.3 0.0 all-gather.4.cloned.1.call-update
  101.3 0.0 all-gather.6.cloned.1.call-start
  101.3 0.7 all-gather.6.cloned.1.call-update
  102.0 0.0 all-gather.8.cloned.1.call-start
  102.1 27.8 %copy.28 = bf16[1024,50,256]{2,1,0:T(8,128)(2,1)} copy(bf16[1024,50,256]{2,0,1:T(8,128)(2,1)} %param.17) | data formatting | bytes 52428800 | tf_op args[8]
  129.9 0.8 dynamic-slice_convert_fusion.1
  130.6 5.3 %fusion.15 = bf16[64,128,256]{2,0,1:T(8,128)(2,1)} fusion(bf16[1024,50,256]{2,1,0:T(8,128)(2,1)} %copy.28, s32[]{:T(128)S(6)} %select_n.16, bf16[64,50]{0,1:T(8,128)(2,1)S(1)} %get-tuple-element.29), kind=kOutput, calls=%fused_computation.14 | convolution fusion | flops 211812352 | bytes 7870724 | tf_op jit(solution)/shard_map/kh,dhc->kdc/dot_general | solution.py:64
  136.0 20.6 %all-gather.4.cloned.1.call-done = bf16[64,64,256]{2,1,0:T(8,128)(2,1)} async-done(((bf16[2,64,256]{2,1,0:T(8,128)(2,1)}), bf16[64,64,256]{2,1,0:T(8,128)(2,1)}) %all-gather.4.cloned.1.call-update) | async-done | bytes 2097168 | tf_op jit(solution)/shard_map/all_gather | solution.py:56
  156.5 5.5 %fusion.22 = bf16[64,64,128]{2,1,0:T(8,128)(2,1)S(1)} fusion(bf16[64,64,256]{2,1,0:T(8,128)(2,1)} %all-gather.4.cloned.1.call-done, bf16[64,128,256]{2,0,1:T(8,128)(2,1)} %fusion.15), kind=kOutput, calls=%fused_computation.27 | convolution fusion | flops 268959744 | bytes 7340032 | tf_op jit(solution)/shard_map/krc,kdc->krd/dot_general | solution.py:66
  162.1 0.2 bitcast_convert_fusion
  162.3 1.8 copy.32
  164.1 33.7 %all-gather.6.cloned.1.call-done = bf16[64,64,128]{2,1,0:T(8,128)(2,1)} async-done(((bf16[8,64,128]{2,1,0:T(8,128)(2,1)}), bf16[64,64,128]{2,1,0:T(8,128)(2,1)}) %all-gather.6.cloned.1.call-update) | async-done | bytes 1048592 | tf_op jit(solution)/shard_map/all_gather | solution.py:39
  197.8 4.2 %convert_reduce_fusion = (f32[128]{0:T(128)S(1)}, bf16[4096,128]{0,1:T(8,128)(2,1)S(1)}, bf16[4096,128]{0,1:T(8,128)(2,1)}) fusion(f32[4096,128]{0,1:T(8,128)} %copy.32, f32[128]{0:T(128)S(1)} %dynamic-slice_convert_fusion.1, bf16[4096,128]{1,0:T(8,128)(2,1)} %bitcast.58, bf16[128,4096]{1,0:T(8,128)(2,1)S(1)} %copy-done, s32[]{:T(128)S(6)} %select_n.17), kind=kOutput, calls=%fused_computation.23 | convolution fusion | flops 141557632 | bytes 5276676 | tf_op jit(solution)/shard_map/dot_general | solution.py:62
  202.1 0.5 convolution_bitcast_fusion
  202.6 0.6 pad_maximum_fusion
  203.2 0.0 all-gather.8.cloned.1.call-update
  203.2 2.3 copy.33
  205.5 2.5 convolution_convert_fusion
  208.0 3.3 %fusion.12 = f32[128,50,256]{2,1,0:T(8,128)S(1)} fusion(bf16[64,128,256]{2,1,0:T(8,128)(2,1)S(1)} %convolution_convert_fusion, bf16[64,50]{0,1:T(8,128)(2,1)S(1)} %get-tuple-element.29), kind=kOutput, calls=%fused_computation.13 | convolution fusion | flops 209715200 | bytes 10754304 | tf_op jit(solution)/shard_map/kh,kdc->dhc/dot_general | solution.py:72
  211.3 4.8 %copy.37 = f32[128,50,256]{2,0,1:T(8,128)} copy(f32[128,50,256]{2,1,0:T(8,128)S(1)} %fusion.12) | data formatting | bytes 13107200
  216.1 7.1 %fusion.25 = f32[64,50]{0,1:T(8,128)S(1)} fusion(bf16[1024,50,256]{2,1,0:T(8,128)(2,1)} %copy.28, s32[]{:T(128)S(6)} %select_n.16, bf16[64,128,256]{2,1,0:T(8,128)(2,1)S(1)} %convolution_convert_fusion), kind=kOutput, calls=%fused_computation.29 | convolution fusion | flops 209715200 | bytes 7877124 | tf_op jit(solution)/shard_map/kdc,dhc->kh/dot_general | solution.py:73
  223.2 39.1 %psum.7 = f32[64,50]{0,1:T(8,128)S(1)} all-reduce(f32[64,50]{0,1:T(8,128)S(1)} %fusion.25), channel_id=1, replica_groups=mesh['dp'=8,'hyper'=4] {'dp','hyper'}, use_global_device_ids=true, to_apply=%region_4.5 | all-reduce | flops 3200 | bytes 25600 | tf_op jit(solution)/shard_map/psum | solution.py:74
  262.3 0.6 fusion.45
  263.0 0.2 fusion.46
  263.2 0.9 fusion.32
  264.1 0.8 fusion.47
  264.9 1.5 slice.9
  266.4 3.1 %slice.8 = f32[128,4096]{1,0:T(8,128)} slice(f32[129,4096]{1,0:T(8,128)} %all-gather.8.cloned.1.call-done), slice={[0:128], [0:4096]} | slice | bytes 4194304 | tf_op jit(solution)/shard_map/slice | solution.py:82
  (11 shorter events, 0.1 us)
Async XLA Ops:
  7.2 51.5 %copy-start = (bf16[128,4096]{1,0:T(8,128)(2,1)S(1)}, bf16[128,4096]{1,0:T(8,128)(2,1)}, u32[]{:S(2)}) copy-start(bf16[128,4096]{1,0:T(8,128)(2,1)} %param.12) | copy-start | bytes 3145732
  7.2 149.4 %all-gather.4.cloned.1.call-start = ((), (), s32[]{:S(2)}) async-start(), calls=%async_computation.1 | async-start | bytes 2162688 | tf_op jit(solution)/shard_map/all_gather | solution.py:56
  56.1 3.2 %copy-start.3 = (bf16[8,64,128]{2,1,0:T(8,128)(2,1)}, bf16[8,64,128]{2,1,0:T(8,128)(2,1)S(1)}, u32[]{:S(2)}) copy-start(bf16[8,64,128]{2,1,0:T(8,128)(2,1)S(1)} %all_gather.15) | copy-start | bytes 393220
  87.4 13.1 %copy-start.5 = (s32[2,64]{1,0:T(2,128)S(1)}, s32[2,64]{1,0:T(2,128)}, u32[]{:S(2)}) copy-start(s32[2,64]{1,0:T(2,128)} %param.10) | copy-start | bytes 1540
  101.3 96.5 %all-gather.6.cloned.1.call-start = ((), (), s32[]{:S(2)}) async-start(), calls=%async_computation.2 | async-start | bytes 1179648 | tf_op jit(solution)/shard_map/all_gather | solution.py:39
  102.0 162.8 %all-gather.8.cloned.1.call-start = ((), (), s32[]{:S(2)}) async-start(), calls=%async_computation.3 | async-start | bytes 2297856 | tf_op jit(solution)/shard_map/all_gather | solution.py:81
  197.8 4.2 %copy-start.2 = (bf16[64,64,128]{2,1,0:T(8,128)(2,1)S(1)}, bf16[64,64,128]{2,1,0:T(8,128)(2,1)}, u32[]{:S(2)}) copy-start(bf16[64,64,128]{2,1,0:T(8,128)(2,1)} %all-gather.6.cloned.1.call-done) | copy-start | bytes 3145732
  202.1 3.4 %copy-start.1 = (bf16[64,64,256]{2,1,0:T(8,128)(2,1)S(1)}, bf16[64,64,256]{2,1,0:T(8,128)(2,1)}, u32[]{:S(2)}) copy-start(bf16[64,64,256]{2,1,0:T(8,128)(2,1)} %all-gather.4.cloned.1.call-done) | copy-start | bytes 6291460
  216.1 46.9 %copy-start.4 = (bf16[128,50]{0,1:T(8,128)(2,1)S(1)}, bf16[128,50]{0,1:T(8,128)(2,1)}, u32[]{:S(2)}) copy-start(bf16[128,50]{0,1:T(8,128)(2,1)} %param.15) | copy-start | bytes 38404
Sparse Core Ops, SparseCore 0:
  101.4 55.0 all-gather.3
  158.7 39.1 all-gather.5
  203.4 56.2 all-gather.7
where the time goes:
time: 277 us; the launch traced here: 276 us
  blocking collectives  98.8 us (36%)
  matrix products  61.7 us (22%)
  waiting for transfers between devices  55.1 us (20%)
  local copies, waits for them, and re-layouts  42.4 us (15%)
  between operations  13.9 us (5%)
  other arithmetic  4 us (1%)
    unnamed x1, blocking collectives  42 us
    psum x1, blocking collectives, local(): dhidden = lax.psum(dhidden, everyone)  39.1 us
    all_gather x1, waiting for transfers between devices, local(): in_all = lax.all_gather(in_group, 'dp', axis=0, tiled=True)  33.7 us
    unnamed x16, local copies, waits for them, and re-layouts  33.5 us
    dot_general x1, matrix products, local(): jnp.einsum('kh,dhc->kdc', hidden_group, hyper_out, preferred_element_type...  28 us
    all_gather x1, waiting for transfers between devices, local(): dl_all = lax.all_gather(dlogits, everyone, axis=0, tiled=True)  20.6 us
    all_to_all x1, blocking collectives, local(): lax.all_to_all(part.reshape(n_hyper, own * rows, classes), 'hyper', split...  11.8 us
    dot_general x1, matrix products, local(): jnp.einsum('kdc,dhc->kh', dheads, out_rows, preferred_element_type=f32)  7.1 us
  transfers between devices with their start and end apart: 3, of which 2 were waited for; matrix products, arithmetic and copies ran while one was open for 23% of the time, Pallas kernels for 0%

commit v1 on v0

--- a/solution.py
+++ b/solution.py
@@ -6,6 +6,24 @@
 highest = lax.Precision.HIGHEST
 f32 = jnp.float32
 bf16 = jnp.bfloat16
+
+
+def edit_ratios_all(unit, which_dim):
+    unit = jnp.moveaxis(unit, 0, which_dim)
+    r1 = unit.shape
+    return unit.reshape(*r1[:which_dim], r1[which_dim] * r1[which_dim + 1], *r1[which_dim + 2 :])
+
+
+def return_all_terms(array_in, which_axis, dim_at):
+    num_devices = lax.axis_size(which_axis)
+    heap = [(num, (num + 1) % num_devices) for num in range(num_devices)]
+    buffers = [array_in]
+    while len(buffers) < num_devices:
+        tile_out = lax.ppermute(buffers[-1], which_axis, heap)
+        buffers.append(tile_out)
+    e_next = lax.axis_index(which_axis)
+    buffers = jnp.stack(buffers)[(e_next - jnp.arange(num_devices)) % num_devices]
+    return edit_ratios_all(buffers, dim_at)
 
 
 def silu_slope(values):
@@ -36,7 +54,7 @@
     classes = hyper_out.shape[2]
     ids = lax.all_gather(client_ids, everyone, axis=0, tiled=True)
     in_group = lax.all_gather(inputs, "hyper", axis=0, tiled=True)
-    in_all = lax.all_gather(in_group, "dp", axis=0, tiled=True)
+    in_all = return_all_terms(in_group, "dp", 0)
     select = ids[:, None] == jnp.arange(embeddings.shape[0], dtype=jnp.int32)[None, :]
     picked = jnp.dot(select.astype(bf16), embeddings, preferred_element_type=f32).astype(bf16)
     hyper_preact = jnp.dot(picked, hyper_in, preferred_element_type=f32) + hyper_bias

time: 277 us -> 255 us (0.921)
  local copies, waits for them, and re-layouts: 42.4 us -> 26.5 us
  waiting for transfers between devices: 55.1 us -> 49.5 us
  starting transfers between devices: 0.12 us -> 3.16 us
  matrix products: 61.7 us -> 58.7 us
    ppermute x0 -> x7, waiting for transfers between devices: none -> 49.4 us  [return_all_terms(): tile_out = lax.ppermute(buffers[-1], which_axis, heap)]
    all_gather x1 -> x0, waiting for transfers between devices: 33.7 us -> none  [local(): in_all = lax.all_gather(in_group, 'dp', axis=0, tiled=True)]
    unnamed x16 -> x29, local copies, waits for them, and re-layouts: 33.5 us -> 12.3 us
    all_gather x1, waiting for transfers between devices: 20.6 us -> 0.02 us  [local(): dl_all = lax.all_gather(dlogits, everyone, axis=0, tiled=True)]
    dot_general x1, matrix products: 7.1 us -> 1.26 us  [local(): jnp.einsum('kdc,dhc->kh', dheads, out_rows, preferred_element_type=f32)]
    ppermute x0 -> x7, starting transfers between devices: none -> 3.08 us  [return_all_terms(): tile_out = lax.ppermute(buffers[-1], which_axis, heap)]
    convert_element_type x2 -> x1, local copies, waits for them, and re-layouts: 4.08 us -> 6.53 us  [local(): jnp.einsum('krd,krc->kdc', features, dl_all, preferred_element_type=f32)]
  transfers between devices with their start and end apart: 3 -> 9, of which waited for: 2 -> 6; matrix products, arithmetic and copies ran while one was open for 23% -> 15% of each run, Pallas kernels for 0% -> 0%
where the time goes in v1:
time: 255 us; the launch traced here: 254 us
  blocking collectives  98.2 us (39%)
  matrix products  58.7 us (23%)
  waiting for transfers between devices  49.5 us (19%)
  local copies, waits for them, and re-layouts  26.5 us (10%)
  between operations  14.3 us (6%)
  other arithmetic  3.82 us (1%)
  starting transfers between devices  3.16 us (1%)
    ppermute x7, waiting for transfers between devices, return_all_terms(): tile_out = lax.ppermute(buffers[-1], which_axis, heap)  49.4 us
    unnamed x1, blocking collectives  42 us
    psum x1, blocking collectives, local(): dhidden = lax.psum(dhidden, everyone)  38.5 us
    dot_general x1, matrix products, local(): jnp.einsum('kh,dhc->kdc', hidden_group, hyper_out, preferred_element_type...  27.9 us
    unnamed x29, local copies, waits for them, and re-layouts  12.3 us
    all_to_all x1, blocking collectives, local(): lax.all_to_all(part.reshape(n_hyper, own * rows, classes), 'hyper', split...  11.8 us
    convert_element_type x1, local copies, waits for them, and re-layouts, local(): jnp.einsum('krd,krc->kdc', features, dl_all, preferred_element_type=f32)  6.53 us
    all_gather x1, blocking collectives, local(): in_group = lax.all_gather(inputs, 'hyper', axis=0, tiled=True)  6.01 us
  transfers between devices with their start and end apart: 9, of which 6 were waited for; matrix products, arithmetic and copies ran while one was open for 15% of the time, Pallas kernels for 0%

profile of v1, /device:TPU:0, one launch (start us, length us, event | category | flops | bytes accessed | tf_op | source)
XLA Modules:
  0.0 254.1 jit_solution(4596444485275928330)
XLA Ops:
  7.2 0.0 all-gather.3.cloned.1.call-start
  7.2 0.9 dynamic-update-slice
  8.2 42.0 %all-reduce = s32[64]{0:T(128)S(1)} all-reduce(s32[64]{0:T(128)S(1)} %dynamic-update-slice), channel_id=1, replica_groups=mesh['dp'=8,'hyper'=4] {'dp','hyper'}, use_global_device_ids=true, to_apply=%add | all-reduce | flops 64 | bytes 512
  50.1 6.0 %all_gather.12 = bf16[8,64,128]{2,1,0:T(8,128)(2,1)S(1)} all-gather(bf16[2,64,128]{2,1,0:T(8,128)(2,1)} %param.9), channel_id=1, replica_groups=mesh['dp'=8,'hyper'=4] {'hyper'}, dimensions={0}, use_global_device_ids=true | all-gather | bytes 163840 | tf_op jit(solution)/shard_map/all_gather | solution.py:56
  56.1 0.7 dynamic-slice_convert_fusion
  56.8 0.9 convolution_convert_fusion.1
  57.7 0.9 multiply_convert_fusion.2
  58.6 1.7 fusion.15
  60.3 27.9 %fusion = bf16[8,1024,256]{2,0,1:T(8,128)(2,1)S(1)} fusion(bf16[1024,50,256]{2,0,1:T(8,128)(2,1)} %param.17, bf16[64,50]{0,1:T(8,128)(2,1)S(1)} %get-tuple-element.23, s32[]{:T(128)S(6)} %select_n.41), kind=kOutput, calls=%fused_computation.1 | convolution fusion | flops 209715200 | bytes 30415108 | tf_op jit(solution)/shard_map/kh,dhc->kdc/dot_general | solution.py:67
  88.2 2.1 fusion.2
  90.3 11.8 %all_to_all.5 = f32[4,128,256]{2,1,0:T(8,128)S(1)} all-to-all(f32[4,128,256]{2,1,0:T(8,128)S(1)} %bitcast.78), channel_id=1, replica_groups=mesh['dp'=8,'hyper'=4] {'hyper'}, dimensions={0} | all-to-all | bytes 1048576 | tf_op jit(solution)/shard_map/all_to_all | solution.py:69
  102.1 0.1 reduce_max.9
  102.2 0.2 exponential_reduce_fusion
  102.4 0.1 sub.39
  102.5 0.1 div.32
  102.6 0.8 multiply_convert_fusion.1
  103.3 0.0 all-gather.3.cloned.1.call-update
  103.4 0.0 all-gather.5.cloned.1.call-start
  103.4 1.4 collective-permute-start
  104.8 2.2 constant_dynamic-slice_fusion
  107.0 5.1 %fusion.6 = bf16[64,128,256]{2,0,1:T(8,128)(2,1)} fusion(bf16[128,50,256]{2,0,1:T(8,128)(2,1)S(1)} %constant_dynamic-slice_fusion, bf16[64,50]{0,1:T(8,128)(2,1)S(1)} %get-tuple-element.23), kind=kOutput, calls=%fused_computation.10 | convolution fusion | flops 209715200 | bytes 7477504 | tf_op jit(solution)/shard_map/kh,dhc->kdc/dot_general | solution.py:82
  112.1 0.8 dynamic-slice_convert_fusion.1
  112.8 1.7 collective-permute-start.1
  114.5 6.5 %collective-permute-done.1 = bf16[8,64,128]{2,1,0:T(8,128)(2,1)S(1)} collective-permute-done((bf16[8,64,128]{2,1,0:T(8,128)(2,1)S(1)}, bf16[8,64,128]{2,1,0:T(8,128)(2,1)S(1)}, u32[]{:S(2)}, u32[]{:S(2)}) %collective-permute-start.1) | collective-permute-done | bytes 131104 | tf_op jit(solution)/shard_map/ppermute | solution.py:22
  121.1 7.6 %collective-permute-done.2 = bf16[8,64,128]{2,1,0:T(8,128)(2,1)S(1)} collective-permute-done((bf16[8,64,128]{2,1,0:T(8,128)(2,1)S(1)}, bf16[8,64,128]{2,1,0:T(8,128)(2,1)S(1)}, u32[]{:S(2)}, u32[]{:S(2)}) %collective-permute-start.2) | collective-permute-done | bytes 131104 | tf_op jit(solution)/shard_map/ppermute | solution.py:22
  128.7 8.2 %collective-permute-done.3 = bf16[8,64,128]{2,1,0:T(8,128)(2,1)S(1)} collective-permute-done((bf16[8,64,128]{2,1,0:T(8,128)(2,1)S(1)}, bf16[8,64,128]{2,1,0:T(8,128)(2,1)S(1)}, u32[]{:S(2)}, u32[]{:S(2)}) %collective-permute-start.3) | collective-permute-done | bytes 131104 | tf_op jit(solution)/shard_map/ppermute | solution.py:22
  136.9 7.8 %collective-permute-done.4 = bf16[8,64,128]{2,1,0:T(8,128)(2,1)S(1)} collective-permute-done((bf16[8,64,128]{2,1,0:T(8,128)(2,1)S(1)}, bf16[8,64,128]{2,1,0:T(8,128)(2,1)S(1)}, u32[]{:S(2)}, u32[]{:S(2)}) %collective-permute-start.4) | collective-permute-done | bytes 131104 | tf_op jit(solution)/shard_map/ppermute | solution.py:22
  144.8 11.7 %collective-permute-done.5 = bf16[8,64,128]{2,1,0:T(8,128)(2,1)S(1)} collective-permute-done((bf16[8,64,128]{2,1,0:T(8,128)(2,1)S(1)}, bf16[8,64,128]{2,1,0:T(8,128)(2,1)S(1)}, u32[]{:S(2)}, u32[]{:S(2)}) %collective-permute-start.5) | collective-permute-done | bytes 131104 | tf_op jit(solution)/shard_map/ppermute | solution.py:22
  156.4 7.6 %collective-permute-done.6 = bf16[8,64,128]{2,1,0:T(8,128)(2,1)S(1)} collective-permute-done((bf16[8,64,128]{2,1,0:T(8,128)(2,1)S(1)}, bf16[8,64,128]{2,1,0:T(8,128)(2,1)S(1)}, u32[]{:S(2)}, u32[]{:S(2)}) %collective-permute-start.6) | collective-permute-done | bytes 131104 | tf_op jit(solution)/shard_map/ppermute | solution.py:22
  164.1 0.7 gather_fusion
  164.9 0.0 all-gather.3.cloned.1.call-done
  164.9 5.5 %fusion.16 = bf16[64,64,128]{2,1,0:T(8,128)(2,1)S(1)} fusion(bf16[64,64,256]{2,1,0:T(8,128)(2,1)} %all-gather.3.cloned.1.call-done, bf16[64,128,256]{2,0,1:T(8,128)(2,1)} %fusion.6), kind=kOutput, calls=%fused_computation.25 | convolution fusion | flops 268959744 | bytes 7340032 | tf_op jit(solution)/shard_map/krc,kdc->krd/dot_general | solution.py:84
  170.4 2.3 convert_reduce_fusion
  172.7 0.5 fusion.33
  173.2 0.6 pad_maximum_fusion
  173.9 6.4 %copy.27 = bf16[128,50,256]{0,1,2:T(8,128)(2,1)} copy(bf16[128,50,256]{2,0,1:T(8,128)(2,1)} %copy-done.2) | data formatting | bytes 6553600
  180.3 3.3 %convolution_convert_fusion = bf16[64,128,256]{2,1,0:T(8,128)(2,1)} fusion(bf16[64,64,128]{2,1,0:T(8,128)(2,1)S(1)} %bitcast.76, bf16[64,64,256]{2,1,0:T(8,128)(2,1)S(1)} %copy-done.5), kind=kOutput, calls=%fused_computation.13 | convolution fusion | flops 270532608 | bytes 7340032 | tf_op jit(solution)/shard_map/krd,krc->kdc/dot_general | solution.py:83
  183.6 6.5 %copy.20 = bf16[64,128,256]{1,0,2:T(8,128)(2,1)} copy(bf16[64,128,256]{2,1,0:T(8,128)(2,1)} %convolution_convert_fusion) | data formatting | bytes 8388608 | tf_op jit(solution)/shard_map/convert_element_type | solution.py:83
  190.1 5.4 %fusion.8 = f32[128,50,256]{2,1,0:T(8,128)S(1)} fusion(bf16[64,128,256]{2,1,0:T(8,128)(2,1)} %convolution_convert_fusion, bf16[64,50]{0,1:T(8,128)(2,1)S(1)} %get-tuple-element.23), kind=kOutput, calls=%fused_computation.12 | convolution fusion | flops 209715200 | bytes 10754304 | tf_op jit(solution)/shard_map/kh,kdc->dhc/dot_general | solution.py:90
  195.6 4.8 %copy.22 = f32[128,50,256]{2,0,1:T(8,128)} copy(f32[128,50,256]{2,1,0:T(8,128)S(1)} %fusion.8) | data formatting | bytes 13107200
  200.4 1.3 convolution_bitcast_fusion
  201.6 38.5 %psum.7 = f32[64,50]{0,1:T(8,128)S(1)} all-reduce(f32[64,50]{0,1:T(8,128)S(1)} %convolution_bitcast_fusion), channel_id=1, replica_groups=mesh['dp'=8,'hyper'=4] {'dp','hyper'}, use_global_device_ids=true, to_apply=%region_4.5 | all-reduce | flops 3200 | bytes 25600 | tf_op jit(solution)/shard_map/psum | solution.py:92
  240.1 0.6 fusion.31
  240.7 0.2 fusion.34
  241.0 0.9 fusion.19
  241.9 0.8 fusion.35
  242.6 1.5 slice.11
  244.2 3.1 %slice.10 = f32[128,4096]{1,0:T(8,128)} slice(f32[129,4096]{1,0:T(8,128)} %all-gather.5.cloned.1.call-done), slice={[0:128], [0:4096]} | slice | bytes 4194304 | tf_op jit(solution)/shard_map/slice | solution.py:100
  (38 shorter events, 0.3 us)
Async XLA Ops:
  7.2 51.5 %copy-start = (bf16[128,4096]{1,0:T(8,128)(2,1)S(1)}, bf16[128,4096]{1,0:T(8,128)(2,1)}, u32[]{:S(2)}) copy-start(bf16[128,4096]{1,0:T(8,128)(2,1)} %param.12) | copy-start | bytes 3145732
  7.2 157.7 %all-gather.3.cloned.1.call-start = ((), (), s32[]{:S(2)}) async-start(), calls=%async_computation.1 | async-start | bytes 2162688 | tf_op jit(solution)/shard_map/all_gather | solution.py:74
  88.2 14.4 %copy-start.8 = (s32[2,64]{1,0:T(2,128)S(1)}, s32[2,64]{1,0:T(2,128)}, u32[]{:S(2)}) copy-start(s32[2,64]{1,0:T(2,128)} %param.10) | copy-start | bytes 1540
  103.4 139.3 %all-gather.5.cloned.1.call-start = ((), (), s32[]{:S(2)}) async-start(), calls=%async_computation.2 | async-start | bytes 2297856 | tf_op jit(solution)/shard_map/all_gather | solution.py:99
  103.4 9.4 %collective-permute-start = (bf16[8,64,128]{2,1,0:T(8,128)(2,1)S(1)}, bf16[8,64,128]{2,1,0:T(8,128)(2,1)S(1)}, u32[]{:S(2)}, u32[]{:S(2)}) collective-permute-start(bf16[8,64,128]{2,1,0:T(8,128)(2,1)S(1)} %all_gather.12), channel_id=1, source_target_pairs={{0,4},{4,8},{8,12},{12,16},{16,20},{20,24},{24,28},{28,0},{1,5},{5... | collective-permute-start | bytes 393224 | tf_op jit(solution)/shard_map/ppermute | solution.py:22
  107.0 5.1 %copy-start.2 = (bf16[128,50,256]{2,0,1:T(8,128)(2,1)}, bf16[128,50,256]{2,0,1:T(8,128)(2,1)S(1)}, u32[]{:S(2)}) copy-start(bf16[128,50,256]{2,0,1:T(8,128)(2,1)S(1)} %constant_dynamic-slice_fusion) | copy-start | bytes 9830404
  112.8 8.2 %collective-permute-start.1 = (bf16[8,64,128]{2,1,0:T(8,128)(2,1)S(1)}, bf16[8,64,128]{2,1,0:T(8,128)(2,1)S(1)}, u32[]{:S(2)}, u32[]{:S(2)}) collective-permute-start(bf16[8,64,128]{2,1,0:T(8,128)(2,1)S(1)} %collective-permute-done), channel_id=1, source_target_pairs={{0,4},{4,8},{8,12},{12,16},{16,20},{20,24},{24,28},{28,0},{1,5},{5... | collective-permute-start | bytes 393224 | tf_op jit(solution)/shard_map/ppermute | solution.py:22
  121.0 7.7 %collective-permute-start.2 = (bf16[8,64,128]{2,1,0:T(8,128)(2,1)S(1)}, bf16[8,64,128]{2,1,0:T(8,128)(2,1)S(1)}, u32[]{:S(2)}, u32[]{:S(2)}) collective-permute-start(bf16[8,64,128]{2,1,0:T(8,128)(2,1)S(1)} %collective-permute-done.1), channel_id=1, source_target_pairs={{0,4},{4,8},{8,12},{12,16},{16,20},{20,24},{24,28},{28,0},{1,5},{5... | collective-permute-start | bytes 393224 | tf_op jit(solution)/shard_map/ppermute | solution.py:22
  128.7 8.2 %collective-permute-start.3 = (bf16[8,64,128]{2,1,0:T(8,128)(2,1)S(1)}, bf16[8,64,128]{2,1,0:T(8,128)(2,1)S(1)}, u32[]{:S(2)}, u32[]{:S(2)}) collective-permute-start(bf16[8,64,128]{2,1,0:T(8,128)(2,1)S(1)} %collective-permute-done.2), channel_id=1, source_target_pairs={{0,4},{4,8},{8,12},{12,16},{16,20},{20,24},{24,28},{28,0},{1,5},{5... | collective-permute-start | bytes 393224 | tf_op jit(solution)/shard_map/ppermute | solution.py:22
  136.9 7.9 %collective-permute-start.4 = (bf16[8,64,128]{2,1,0:T(8,128)(2,1)S(1)}, bf16[8,64,128]{2,1,0:T(8,128)(2,1)S(1)}, u32[]{:S(2)}, u32[]{:S(2)}) collective-permute-start(bf16[8,64,128]{2,1,0:T(8,128)(2,1)S(1)} %collective-permute-done.3), channel_id=1, source_target_pairs={{0,4},{4,8},{8,12},{12,16},{16,20},{20,24},{24,28},{28,0},{1,5},{5... | collective-permute-start | bytes 393224 | tf_op jit(solution)/shard_map/ppermute | solution.py:22
  144.7 11.7 %collective-permute-start.5 = (bf16[8,64,128]{2,1,0:T(8,128)(2,1)S(1)}, bf16[8,64,128]{2,1,0:T(8,128)(2,1)S(1)}, u32[]{:S(2)}, u32[]{:S(2)}) collective-permute-start(bf16[8,64,128]{2,1,0:T(8,128)(2,1)S(1)} %collective-permute-done.4), channel_id=1, source_target_pairs={{0,4},{4,8},{8,12},{12,16},{16,20},{20,24},{24,28},{28,0},{1,5},{5... | collective-permute-start | bytes 393224 | tf_op jit(solution)/shard_map/ppermute | solution.py:22
  156.4 7.7 %collective-permute-start.6 = (bf16[8,64,128]{2,1,0:T(8,128)(2,1)S(1)}, bf16[8,64,128]{2,1,0:T(8,128)(2,1)S(1)}, u32[]{:S(2)}, u32[]{:S(2)}) collective-permute-start(bf16[8,64,128]{2,1,0:T(8,128)(2,1)S(1)} %collective-permute-done.5), channel_id=1, source_target_pairs={{0,4},{4,8},{8,12},{12,16},{16,20},{20,24},{24,28},{28,0},{1,5},{5... | collective-permute-start | bytes 393224 | tf_op jit(solution)/shard_map/ppermute | solution.py:22
  173.9 6.4 %copy-start.5 = (bf16[64,64,256]{2,1,0:T(8,128)(2,1)S(1)}, bf16[64,64,256]{2,1,0:T(8,128)(2,1)}, u32[]{:S(2)}) copy-start(bf16[64,64,256]{2,1,0:T(8,128)(2,1)} %all-gather.3.cloned.1.call-done) | copy-start | bytes 6291460
  173.9 6.4 %copy-start.6 = (bf16[4096,128]{1,0:T(8,128)(2,1)S(1)}, bf16[4096,128]{1,0:T(8,128)(2,1)}, u32[]{:S(2)}) copy-start(bf16[4096,128]{1,0:T(8,128)(2,1)} %get-tuple-element.22) | copy-start | bytes 3145732
  195.5 4.8 %copy-start.3 = (bf16[64,128,256]{1,0,2:T(8,128)(2,1)S(1)}, bf16[64,128,256]{1,0,2:T(8,128)(2,1)}, u32[]{:S(2)}) copy-start(bf16[64,128,256]{1,0,2:T(8,128)(2,1)} %copy.20) | copy-start | bytes 12582916
  195.5 4.8 %copy-start.4 = (bf16[128,50,256]{0,1,2:T(8,128)(2,1)S(1)}, bf16[128,50,256]{0,1,2:T(8,128)(2,1)}, u32[]{:S(2)}) copy-start(bf16[128,50,256]{0,1,2:T(8,128)(2,1)} %copy.27) | copy-start | bytes 9830404
  200.3 40.4 %copy-start.7 = (bf16[128,50]{0,1:T(8,128)(2,1)S(1)}, bf16[128,50]{0,1:T(8,128)(2,1)}, u32[]{:S(2)}) copy-start(bf16[128,50]{0,1:T(8,128)(2,1)} %param.15) | copy-start | bytes 38404
  200.4 46.9 %copy-start.1 = (bf16[128,4096]{1,0:T(8,128)(2,1)S(1)}, bf16[128,4096]{1,0:T(8,128)(2,1)}, u32[]{:S(2)}) copy-start(bf16[128,4096]{1,0:T(8,128)(2,1)} %param.12) | copy-start | bytes 3145732
Sparse Core Ops, SparseCore 0:
  103.5 58.2 all-gather.2
  174.0 54.0 all-gather.4
